TPU v7x, 32 devices: a whole 2x2x4 slice. The times are simulated.
32 devices in a mesh: dp: 2 (over y), expert: 16 (over z, x, core).
Axes of the slice: x: 2, y: 2, z: 4, core: 2. Of those that a mesh axis runs over, the one named last changes fastest.
Arguments:
- tokens: bfloat16 [256, 2880], P(('dp', 'expert')), may hold values from -6 to 6
- routes: int32 [2, 256, 4], P(None, ('dp', 'expert')), may hold values from 0 to 15, all different within a row; in each aligned block of 8 rows (0 to 7, 8 to 15, ..., all dimensions but the last counted through in order) at most 4 rows name the same one
- placement: int32 [2, 16], replicated, may hold values from 0 to 15, each once within a row
- up_weight: bfloat16 [2, 16, 2880, 1440], P(None, 'expert', None, 'dp'), may hold values from -0.109375 to 0.109375
- down_weight: bfloat16 [2, 16, 1440, 2880], P(None, 'expert', 'dp'), may hold values from -0.15625 to 0.15625
- router_weight: bfloat16 [2, 16, 2880], P(None, 'expert'), may hold values from -0.21875 to 0.21875
Outputs:
- final_stream: bfloat16 [256, 2880], P(('dp', 'expert'))
Inputs may be any that keep to these rules, and one draw needn't show every extreme that they name: `routes`: each row names 4 different experts. Within one layer's rows of one device no expert is named by more than 4 rows, and some device names some expert exactly 4 times. `placement`: each layer's row is a permutation of the slots.
All inputs are finite; a program needn't handle non-finite values.
Results may differ from a plain program's by a relative error of at most 0.008.
Values may be sent and summed in bfloat16 or wider, within the bound.
A program may use at most 64 MiB of HBM per device.

v0:
```python
import jax
import jax.numpy as jnp
from jax import lax
from jax.sharding import PartitionSpec as P


def rms_rows(stream):
    values = stream.astype(jnp.float32)
    inverse = lax.rsqrt(jnp.mean(values * values, axis=-1, keepdims=True) + 1e-05)
    return (values * inverse).astype(jnp.bfloat16)


def slot_table(route_rows, place_row, columns, capacity):
    tok_rows, top_k = route_rows.shape
    experts = place_row.shape[0]
    matches = route_rows[:, :, None] == jnp.arange(experts, dtype=jnp.int32)[None, None, :]
    target = jnp.sum(jnp.where(matches, place_row[None, None, :], 0), axis=2).reshape(-1)
    row_count = target.shape[0]
    positions = jnp.arange(row_count, dtype=jnp.int32)
    earlier = (positions[None, :] < positions[:, None]) & (target[None, :] == target[:, None])
    row_rank = jnp.sum(earlier.astype(jnp.int32), axis=1)
    placed = (target[:, None, None] == jnp.arange(columns, dtype=jnp.int32)[None, :, None]) & (
        row_rank[:, None, None] == jnp.arange(capacity, dtype=jnp.int32)[None, None, :]
    )
    slot_map = jnp.sum(
        placed.reshape(tok_rows, top_k, columns, capacity).astype(jnp.float32), axis=1
    )
    return jnp.transpose(slot_map, (1, 2, 0))


def per_device(tokens, routes, placement, up_weight, down_weight, router_weight):
    groups = lax.axis_size("dp")
    columns = lax.axis_size("expert")
    tok_rows = tokens.shape[0]
    top_k = routes.shape[2]
    capacity = 2 * tok_rows * top_k // columns

    def layer_step(stream, packed):
        route_rows, place_row, up_part, down_part, router_part = packed
        normed = rms_rows(stream)
        slot_map = slot_table(route_rows, place_row, columns, capacity)
        outgoing = jnp.einsum(
            "jct,td->jcd", slot_map.astype(jnp.bfloat16), normed, preferred_element_type=jnp.float32
        ).astype(jnp.bfloat16)
        arrived = lax.all_to_all(
            outgoing, "expert", split_axis=0, concat_axis=0, tiled=True
        ).reshape(columns * capacity, -1)
        affinity = jax.nn.sigmoid(
            jnp.dot(arrived, router_part[0], preferred_element_type=jnp.float32)
        ).astype(jnp.bfloat16)
        all_rows, all_gates = (
            lax.all_gather(arrived, "dp", axis=0, tiled=True),
            lax.all_gather(affinity, "dp", axis=0, tiled=True),
        )
        hidden = jax.nn.silu(
            jnp.dot(all_rows, up_part[0], preferred_element_type=jnp.float32)
        ).astype(jnp.bfloat16)
        part_sums = jnp.dot(hidden, down_part[0], preferred_element_type=jnp.float32).astype(
            jnp.bfloat16
        )
        part_sums = part_sums.reshape(groups, columns, capacity, -1)
        all_gates = all_gates.reshape(groups, columns, capacity)
        returned, gates_back = (
            lax.all_to_all(
                lax.all_to_all(part_sums, "dp", split_axis=0, concat_axis=0, tiled=True),
                "expert",
                split_axis=1,
                concat_axis=1,
                tiled=True,
            ),
            lax.all_to_all(
                lax.all_to_all(all_gates, "dp", split_axis=0, concat_axis=0, tiled=True),
                "expert",
                split_axis=1,
                concat_axis=1,
                tiled=True,
            ),
        )
        weights = slot_map * gates_back[0].astype(jnp.float32)[:, :, None]
        numerator = jnp.einsum(
            "ect,gecd->td",
            weights.astype(jnp.bfloat16),
            returned,
            preferred_element_type=jnp.float32,
        )
        denominator = jnp.sum(weights, axis=(0, 1))
        updated = stream.astype(jnp.float32) + numerator / jnp.maximum(denominator, 0.5)[:, None]
        return (updated.astype(jnp.bfloat16), None)

    result_stream, unused = lax.scan(
        layer_step, tokens, (routes, placement, up_weight, down_weight, router_weight)
    )
    return result_stream


def solution(mesh):
    return jax.shard_map(
        per_device,
        mesh=mesh,
        in_specs=(
            P(("dp", "expert"), None),
            P(None, ("dp", "expert"), None),
            P(),
            P(None, "expert", None, "dp"),
            P(None, "expert", "dp", None),
            P(None, "expert", None),
        ),
        out_specs=P(("dp", "expert"), None),
        check_vma=False,
    )
```

profile of v0, /device:TPU:0, one launch (start us, length us, event | category | flops | bytes accessed | tf_op | source)
XLA Modules:
  0.0 197.5 jit_solution(17094374580464921686)
XLA Ops:
  0.8 196.1 %while.10 = (s32[]{:T(128)}, bf16[8,2880]{1,0:T(8,128)(2,1)S(1)}, s32[2,8,4]{1,2,0:T(4,128)}, s32[2,16]{1,0:T(2,128)}, bf16[2,1,2880]{2,0,1:T(2,128)(2,1)}, /*in...) while((s32[]{:T(128)}, bf16[8,2880]{1,0:T(8,128)(2,1)S(1)}, ...), condition=%wide.region_7.8_spmd, body=%wide.region_0.7_spmd.sunk | while | flops 1069763072 | bytes 25014808 | solution.py:90
  4.4 7.4 %all-to-all-start = ((bf16[16,4,2880]{2,1,0:T(4,128)(2,1)}), bf16[16,4,2880]{2,1,0:T(4,128)(2,1)S(1)}, u32[]{:S(2)}, u32[]{:S(2)}) async-start(bf16[16,4,2880]{2,1,0:T(4,128)(2,1)} %copy.58), calls=%async_computation | async-start | bytes 753664 | tf_op jit(solution)/shard_map/while/body/eval_jaxpr/all_to_all | solution.py:45
  11.8 1.2 dynamic-slice.2
  13.7 10.0 %all-to-all-done = bf16[16,4,2880]{2,1,0:T(4,128)(2,1)S(1)} async-done(((bf16[16,4,2880]{2,1,0:T(4,128)(2,1)}), bf16[16,4,2880]{2,1,0:T(4,128)(2,1)S(1)}, u32[]{:S(2)}, u32[]{:S(2)}) %all-to-all-start) | async-done | bytes 368672 | tf_op jit(solution)/shard_map/while/body/eval_jaxpr/all_to_all | solution.py:45
  23.9 11.4 %all_gather.7 = bf16[128,2880]{1,0:T(8,128)(2,1)S(1)} all-gather(bf16[64,2880]{1,0:T(8,128)(2,1)S(1)} %reshape.105), channel_id=1, replica_groups=mesh['dp'=2,'expert'=16] {'dp'}, dimensions={0}, use_global_device_ids=true | all-gather | bytes 1105920 | tf_op jit(solution)/shard_map/while/body/eval_jaxpr/all_gather | solution.py:52
  36.5 4.9 %all-reduce.2 = bf16[128]{0:T(256)(128)(2,1)S(1)} all-reduce(bf16[128]{0:T(256)(128)(2,1)S(1)} %dynamic-update-slice.2), channel_id=1, replica_groups=mesh['dp'=2,'expert'=16] {'dp'}, use_global_device_ids=true, to_apply=%add | all-reduce | flops 128 | bytes 512 | tf_op jit(solution)/shard_map/while
  42.2 3.2 %all-to-all-start.3 = ((bf16[2,16,4]{1,2,0:T(4,128)(2,1)}), bf16[2,16,4]{1,2,0:T(4,128)(2,1)S(1)}, u32[]{:S(2)}, u32[]{:S(2)}) async-start(bf16[2,16,4]{1,2,0:T(4,128)(2,1)} %copy.61), calls=%async_computation.3 | async-start | bytes 4096 | tf_op jit(solution)/shard_map/while/body/eval_jaxpr/all_to_all | solution.py:72
  45.4 8.2 %fusion.68 = bf16[128,2880]{0,1:T(8,128)(2,1)S(1)} fusion(bf16[2,1,720,2880]{3,2,1,0:T(8,128)(2,1)} %get-tuple-element.130, s32[]{:T(128)} %get-tuple-element.112, bf16[128,2880]{1,0:T(8,128)(2,1)S(1)} %all_gather.7, bf16[2,1,2880,720]{2,3,1,0:T(8,128)(2,1)} %get-tuple-element.129), kind=kOutput, calls=%fused_computation.6.clone.1 | convolution fusion | flops 1062512640 | bytes 9954304 | tf_op jit(solution)/shard_map/while/body/eval_jaxpr/dot_general | solution.py:58
  54.0 1.1 reshape.106
  55.1 3.5 %all-to-all-start.1 = ((bf16[2,16,4,2880]{3,2,1,0:T(4,128)(2,1)}), bf16[2,16,4,2880]{3,2,1,0:T(4,128)(2,1)S(1)}, u32[]{:S(2)}, u32[]{:S(2)}) async-start(bf16[2,16,4,2880]{3,2,1,0:T(4,128)(2,1)} %reshape.106), calls=%async_computation.1 | async-start | bytes 1507328 | tf_op jit(solution)/shard_map/while/body/eval_jaxpr/all_to_all | solution.py:65
  59.3 8.3 %all-to-all-done.1 = bf16[2,16,4,2880]{3,2,1,0:T(4,128)(2,1)S(1)} async-done(((bf16[2,16,4,2880]{3,2,1,0:T(4,128)(2,1)}), bf16[2,16,4,2880]{3,2,1,0:T(4,128)(2,1)S(1)}, u32[]{:S(2)}, u32[]{:S(2)}) %all-to-all-start.1) | async-done | bytes 737312 | tf_op jit(solution)/shard_map/while/body/eval_jaxpr/all_to_all | solution.py:65
  67.6 3.9 %all-to-all-start.4 = ((bf16[2,16,4]{2,0,1:T(2,128)(2,1)}), bf16[2,16,4]{2,0,1:T(2,128)(2,1)S(1)}, u32[]{:S(2)}, u32[]{:S(2)}) async-start(bf16[2,16,4]{2,0,1:T(2,128)(2,1)} %copy.62), calls=%async_computation.4 | async-start | bytes 16384 | tf_op jit(solution)/shard_map/while/body/eval_jaxpr/all_to_all | solution.py:71
  71.5 1.1 copy.60
  72.6 5.2 %all-to-all-done.4 = bf16[2,16,4]{2,0,1:T(2,128)(2,1)S(1)} async-done(((bf16[2,16,4]{2,0,1:T(2,128)(2,1)}), bf16[2,16,4]{2,0,1:T(2,128)(2,1)S(1)}, u32[]{:S(2)}, u32[]{:S(2)}) %all-to-all-start.4) | async-done | bytes 288 | tf_op jit(solution)/shard_map/while/body/eval_jaxpr/all_to_all | solution.py:71
  77.8 3.6 %all-to-all-start.2 = ((bf16[2,16,4,2880]{3,2,0,1:T(4,128)(2,1)}), bf16[2,16,4,2880]{3,2,0,1:T(4,128)(2,1)S(1)}, u32[]{:S(2)}, u32[]{:S(2)}) async-start(bf16[2,16,4,2880]{3,2,0,1:T(4,128)(2,1)} %copy.60), calls=%async_computation.2 | async-start | bytes 1507328 | tf_op jit(solution)/shard_map/while/body/eval_jaxpr/all_to_all | solution.py:64
  81.7 17.9 %all-to-all-done.2 = bf16[2,16,4,2880]{3,2,0,1:T(4,128)(2,1)S(1)} async-done(((bf16[2,16,4,2880]{3,2,0,1:T(4,128)(2,1)}), bf16[2,16,4,2880]{3,2,0,1:T(4,128)(2,1)S(1)}, u32[]{:S(2)}, u32[]{:S(2)}) %all-to-all-start.2) | async-done | bytes 737312 | tf_op jit(solution)/shard_map/while/body/eval_jaxpr/all_to_all | solution.py:64
  103.6 5.2 %all-to-all-start = ((bf16[16,4,2880]{2,1,0:T(4,128)(2,1)}), bf16[16,4,2880]{2,1,0:T(4,128)(2,1)S(1)}, u32[]{:S(2)}, u32[]{:S(2)}) async-start(bf16[16,4,2880]{2,1,0:T(4,128)(2,1)} %copy.58), calls=%async_computation | async-start | bytes 753664 | tf_op jit(solution)/shard_map/while/body/eval_jaxpr/all_to_all | solution.py:45
  108.8 1.2 dynamic-slice.2
  110.7 10.0 %all-to-all-done = bf16[16,4,2880]{2,1,0:T(4,128)(2,1)S(1)} async-done(((bf16[16,4,2880]{2,1,0:T(4,128)(2,1)}), bf16[16,4,2880]{2,1,0:T(4,128)(2,1)S(1)}, u32[]{:S(2)}, u32[]{:S(2)}) %all-to-all-start) | async-done | bytes 368672 | tf_op jit(solution)/shard_map/while/body/eval_jaxpr/all_to_all | solution.py:45
  120.8 11.4 %all_gather.7 = bf16[128,2880]{1,0:T(8,128)(2,1)S(1)} all-gather(bf16[64,2880]{1,0:T(8,128)(2,1)S(1)} %reshape.105), channel_id=1, replica_groups=mesh['dp'=2,'expert'=16] {'dp'}, dimensions={0}, use_global_device_ids=true | all-gather | bytes 1105920 | tf_op jit(solution)/shard_map/while/body/eval_jaxpr/all_gather | solution.py:52
  132.3 0.9 fusion.69
  133.4 4.9 %all-reduce.2 = bf16[128]{0:T(256)(128)(2,1)S(1)} all-reduce(bf16[128]{0:T(256)(128)(2,1)S(1)} %dynamic-update-slice.2), channel_id=1, replica_groups=mesh['dp'=2,'expert'=16] {'dp'}, use_global_device_ids=true, to_apply=%add | all-reduce | flops 128 | bytes 512 | tf_op jit(solution)/shard_map/while
  139.1 3.2 %all-to-all-start.3 = ((bf16[2,16,4]{1,2,0:T(4,128)(2,1)}), bf16[2,16,4]{1,2,0:T(4,128)(2,1)S(1)}, u32[]{:S(2)}, u32[]{:S(2)}) async-start(bf16[2,16,4]{1,2,0:T(4,128)(2,1)} %copy.61), calls=%async_computation.3 | async-start | bytes 4096 | tf_op jit(solution)/shard_map/while/body/eval_jaxpr/all_to_all | solution.py:72
  142.3 8.2 %fusion.68 = bf16[128,2880]{0,1:T(8,128)(2,1)S(1)} fusion(bf16[2,1,720,2880]{3,2,1,0:T(8,128)(2,1)} %get-tuple-element.130, s32[]{:T(128)} %get-tuple-element.112, bf16[128,2880]{1,0:T(8,128)(2,1)S(1)} %all_gather.7, bf16[2,1,2880,720]{2,3,1,0:T(8,128)(2,1)} %get-tuple-element.129), kind=kOutput, calls=%fused_computation.6.clone.1 | convolution fusion | flops 1062512640 | bytes 9954304 | tf_op jit(solution)/shard_map/while/body/eval_jaxpr/dot_general | solution.py:58
  150.9 1.1 reshape.106
  152.0 3.5 %all-to-all-start.1 = ((bf16[2,16,4,2880]{3,2,1,0:T(4,128)(2,1)}), bf16[2,16,4,2880]{3,2,1,0:T(4,128)(2,1)S(1)}, u32[]{:S(2)}, u32[]{:S(2)}) async-start(bf16[2,16,4,2880]{3,2,1,0:T(4,128)(2,1)} %reshape.106), calls=%async_computation.1 | async-start | bytes 1507328 | tf_op jit(solution)/shard_map/while/body/eval_jaxpr/all_to_all | solution.py:65
  156.2 8.3 %all-to-all-done.1 = bf16[2,16,4,2880]{3,2,1,0:T(4,128)(2,1)S(1)} async-done(((bf16[2,16,4,2880]{3,2,1,0:T(4,128)(2,1)}), bf16[2,16,4,2880]{3,2,1,0:T(4,128)(2,1)S(1)}, u32[]{:S(2)}, u32[]{:S(2)}) %all-to-all-start.1) | async-done | bytes 737312 | tf_op jit(solution)/shard_map/while/body/eval_jaxpr/all_to_all | solution.py:65
  164.5 3.9 %all-to-all-start.4 = ((bf16[2,16,4]{2,0,1:T(2,128)(2,1)}), bf16[2,16,4]{2,0,1:T(2,128)(2,1)S(1)}, u32[]{:S(2)}, u32[]{:S(2)}) async-start(bf16[2,16,4]{2,0,1:T(2,128)(2,1)} %copy.62), calls=%async_computation.4 | async-start | bytes 16384 | tf_op jit(solution)/shard_map/while/body/eval_jaxpr/all_to_all | solution.py:71
  168.4 1.1 copy.60
  169.6 5.2 %all-to-all-done.4 = bf16[2,16,4]{2,0,1:T(2,128)(2,1)S(1)} async-done(((bf16[2,16,4]{2,0,1:T(2,128)(2,1)}), bf16[2,16,4]{2,0,1:T(2,128)(2,1)S(1)}, u32[]{:S(2)}, u32[]{:S(2)}) %all-to-all-start.4) | async-done | bytes 288 | tf_op jit(solution)/shard_map/while/body/eval_jaxpr/all_to_all | solution.py:71
  174.8 3.6 %all-to-all-start.2 = ((bf16[2,16,4,2880]{3,2,0,1:T(4,128)(2,1)}), bf16[2,16,4,2880]{3,2,0,1:T(4,128)(2,1)S(1)}, u32[]{:S(2)}, u32[]{:S(2)}) async-start(bf16[2,16,4,2880]{3,2,0,1:T(4,128)(2,1)} %copy.60), calls=%async_computation.2 | async-start | bytes 1507328 | tf_op jit(solution)/shard_map/while/body/eval_jaxpr/all_to_all | solution.py:64
  178.6 17.9 %all-to-all-done.2 = bf16[2,16,4,2880]{3,2,0,1:T(4,128)(2,1)S(1)} async-done(((bf16[2,16,4,2880]{3,2,0,1:T(4,128)(2,1)}), bf16[2,16,4,2880]{3,2,0,1:T(4,128)(2,1)S(1)}, u32[]{:S(2)}, u32[]{:S(2)}) %all-to-all-start.2) | async-done | bytes 737312 | tf_op jit(solution)/shard_map/while/body/eval_jaxpr/all_to_all | solution.py:64
  (62 shorter events, 15.3 us)
Async XLA Ops:
  4.4 19.3 %all-to-all-start = ((bf16[16,4,2880]{2,1,0:T(4,128)(2,1)}), bf16[16,4,2880]{2,1,0:T(4,128)(2,1)S(1)}, u32[]{:S(2)}, u32[]{:S(2)}) async-start(bf16[16,4,2880]{2,1,0:T(4,128)(2,1)} %copy.58), calls=%async_computation | async-start | bytes 753664 | tf_op jit(solution)/shard_map/while/body/eval_jaxpr/all_to_all | solution.py:45
  42.2 12.9 %all-to-all-start.3 = ((bf16[2,16,4]{1,2,0:T(4,128)(2,1)}), bf16[2,16,4]{1,2,0:T(4,128)(2,1)S(1)}, u32[]{:S(2)}, u32[]{:S(2)}) async-start(bf16[2,16,4]{1,2,0:T(4,128)(2,1)} %copy.61), calls=%async_computation.3 | async-start | bytes 4096 | tf_op jit(solution)/shard_map/while/body/eval_jaxpr/all_to_all | solution.py:72
  55.1 12.5 %all-to-all-start.1 = ((bf16[2,16,4,2880]{3,2,1,0:T(4,128)(2,1)}), bf16[2,16,4,2880]{3,2,1,0:T(4,128)(2,1)S(1)}, u32[]{:S(2)}, u32[]{:S(2)}) async-start(bf16[2,16,4,2880]{3,2,1,0:T(4,128)(2,1)} %reshape.106), calls=%async_computation.1 | async-start | bytes 1507328 | tf_op jit(solution)/shard_map/while/body/eval_jaxpr/all_to_all | solution.py:65
  67.6 10.3 %all-to-all-start.4 = ((bf16[2,16,4]{2,0,1:T(2,128)(2,1)}), bf16[2,16,4]{2,0,1:T(2,128)(2,1)S(1)}, u32[]{:S(2)}, u32[]{:S(2)}) async-start(bf16[2,16,4]{2,0,1:T(2,128)(2,1)} %copy.62), calls=%async_computation.4 | async-start | bytes 16384 | tf_op jit(solution)/shard_map/while/body/eval_jaxpr/all_to_all | solution.py:71
  77.8 21.7 %all-to-all-start.2 = ((bf16[2,16,4,2880]{3,2,0,1:T(4,128)(2,1)}), bf16[2,16,4,2880]{3,2,0,1:T(4,128)(2,1)S(1)}, u32[]{:S(2)}, u32[]{:S(2)}) async-start(bf16[2,16,4,2880]{3,2,0,1:T(4,128)(2,1)} %copy.60), calls=%async_computation.2 | async-start | bytes 1507328 | tf_op jit(solution)/shard_map/while/body/eval_jaxpr/all_to_all | solution.py:64
  103.6 17.0 %all-to-all-start = ((bf16[16,4,2880]{2,1,0:T(4,128)(2,1)}), bf16[16,4,2880]{2,1,0:T(4,128)(2,1)S(1)}, u32[]{:S(2)}, u32[]{:S(2)}) async-start(bf16[16,4,2880]{2,1,0:T(4,128)(2,1)} %copy.58), calls=%async_computation | async-start | bytes 753664 | tf_op jit(solution)/shard_map/while/body/eval_jaxpr/all_to_all | solution.py:45
  139.1 12.9 %all-to-all-start.3 = ((bf16[2,16,4]{1,2,0:T(4,128)(2,1)}), bf16[2,16,4]{1,2,0:T(4,128)(2,1)S(1)}, u32[]{:S(2)}, u32[]{:S(2)}) async-start(bf16[2,16,4]{1,2,0:T(4,128)(2,1)} %copy.61), calls=%async_computation.3 | async-start | bytes 4096 | tf_op jit(solution)/shard_map/while/body/eval_jaxpr/all_to_all | solution.py:72
  152.0 12.5 %all-to-all-start.1 = ((bf16[2,16,4,2880]{3,2,1,0:T(4,128)(2,1)}), bf16[2,16,4,2880]{3,2,1,0:T(4,128)(2,1)S(1)}, u32[]{:S(2)}, u32[]{:S(2)}) async-start(bf16[2,16,4,2880]{3,2,1,0:T(4,128)(2,1)} %reshape.106), calls=%async_computation.1 | async-start | bytes 1507328 | tf_op jit(solution)/shard_map/while/body/eval_jaxpr/all_to_all | solution.py:65
  164.5 10.3 %all-to-all-start.4 = ((bf16[2,16,4]{2,0,1:T(2,128)(2,1)}), bf16[2,16,4]{2,0,1:T(2,128)(2,1)S(1)}, u32[]{:S(2)}, u32[]{:S(2)}) async-start(bf16[2,16,4]{2,0,1:T(2,128)(2,1)} %copy.62), calls=%async_computation.4 | async-start | bytes 16384 | tf_op jit(solution)/shard_map/while/body/eval_jaxpr/all_to_all | solution.py:71
  174.8 21.7 %all-to-all-start.2 = ((bf16[2,16,4,2880]{3,2,0,1:T(4,128)(2,1)}), bf16[2,16,4,2880]{3,2,0,1:T(4,128)(2,1)S(1)}, u32[]{:S(2)}, u32[]{:S(2)}) async-start(bf16[2,16,4,2880]{3,2,0,1:T(4,128)(2,1)} %copy.60), calls=%async_computation.2 | async-start | bytes 1507328 | tf_op jit(solution)/shard_map/while/body/eval_jaxpr/all_to_all | solution.py:64
  196.9 0.6 copy-start
where the time goes:
time: 199 us; the launch traced here: 198 us
  waiting for transfers between devices  82.7 us (42%)
  starting transfers between devices  41.1 us (21%)
  blocking collectives  32.7 us (16%)
  matrix products  19.4 us (10%)
  local copies, waits for them, and re-layouts  18.1 us (9%)
    all_to_all x2, waiting for transfers between devices, layer_step(): lax.all_to_all(lax.all_to_all(part_sums, 'dp', split_axis=0, concat_axis=...  35.8 us
    all_gather x2, blocking collectives, layer_step(): lax.all_gather(arrived, 'dp', axis=0, tiled=True)  22.9 us
    all_to_all x2, waiting for transfers between devices, layer_step(): lax.all_to_all(outgoing, 'expert', split_axis=0, concat_axis=0, tiled=True)  19.9 us
    all_to_all x2, waiting for transfers between devices, layer_step(): lax.all_to_all(part_sums, 'dp', split_axis=0, concat_axis=0, tiled=True)  16.5 us
    dot_general x2, matrix products, layer_step(): jnp.dot(hidden, down_part[0], preferred_element_type=jnp.float32)  16.4 us
    all_to_all x2, starting transfers between devices, layer_step(): lax.all_to_all(outgoing, 'expert', split_axis=0, concat_axis=0, tiled=True)  12.5 us
    all_to_all x2, waiting for transfers between devices, layer_step(): lax.all_to_all(lax.all_to_all(all_gates, 'dp', split_axis=0, concat_axis=...  10.5 us
    while x2, blocking collectives  9.82 us
  transfers between devices with their start and end apart: 10, of which 8 were waited for; matrix products, arithmetic and copies ran while one was open for 13% of the time, Pallas kernels for 0%

commit v1 on v0

--- a/solution.py
+++ b/solution.py
@@ -61,12 +61,22 @@
         part_sums = part_sums.reshape(groups, columns, capacity, -1)
         all_gates = all_gates.reshape(groups, columns, capacity)
         returned, gates_back = (
-            lax.all_to_all(
-                lax.all_to_all(part_sums, "dp", split_axis=0, concat_axis=0, tiled=True),
-                "expert",
-                split_axis=1,
-                concat_axis=1,
-                tiled=True,
+            jnp.concatenate(
+                lax.all_to_all(
+                    jnp.stack(
+                        jnp.split(
+                            lax.all_to_all(
+                                part_sums, "dp", split_axis=0, concat_axis=0, tiled=True
+                            ),
+                            lax.axis_size("expert"),
+                            axis=1,
+                        )
+                    ),
+                    "expert",
+                    0,
+                    0,
+                ),
+                axis=1,
             ),
             lax.all_to_all(
                 lax.all_to_all(all_gates, "dp", split_axis=0, concat_axis=0, tiled=True),

time: 199 us -> 212 us (1.065)
  local copies, waits for them, and re-layouts: 18.1 us -> 36.1 us
  waiting for transfers between devices: 82.7 us -> 72.3 us
  starting transfers between devices: 41.1 us -> 45.9 us
    while x8 -> x38, local copies, waits for them, and re-layouts: 3.18 us -> 22.1 us
    all_to_all x2, waiting for transfers between devices: 10.5 us -> 0.01 us  [layer_step(): lax.all_to_all(lax.all_to_all(all_gates, 'dp', split_axis=0, concat_axis=...]
    all_to_all x2, starting transfers between devices: 7.22 us -> 12 us  [layer_step(): lax.all_to_all(jnp.stack(jnp.split(lax.all_to_all(part_sums, 'dp', split_...]
    all_to_all x2 -> x0, local copies, waits for them, and re-layouts: 2.26 us -> none  [layer_step(): lax.all_to_all(part_sums, 'dp', split_axis=0, concat_axis=0, tiled=True)]
  transfers between devices with their start and end apart: 10 -> 10, of which waited for: 8 -> 6; matrix products, arithmetic and copies ran while one was open for 13% -> 21% of each run, Pallas kernels for 0% -> 0%
where the time goes in v1:
time: 212 us; the launch traced here: 211 us
  waiting for transfers between devices  72.3 us (34%)
  starting transfers between devices  45.9 us (22%)
  local copies, waits for them, and re-layouts  36.1 us (17%)
  blocking collectives  32.7 us (15%)
  matrix products  19.4 us (9%)
  other arithmetic  2.67 us (1%)
    all_to_all x2, waiting for transfers between devices, layer_step(): lax.all_to_all(jnp.stack(jnp.split(lax.all_to_all(part_sums, 'dp', split_...  35.8 us
    all_gather x2, blocking collectives, layer_step(): lax.all_gather(arrived, 'dp', axis=0, tiled=True)  22.9 us
    while x38, local copies, waits for them, and re-layouts  22.1 us
    all_to_all x2, waiting for transfers between devices, layer_step(): lax.all_to_all(outgoing, 'expert', split_axis=0, concat_axis=0, tiled=True)  19.9 us
    all_to_all x2, waiting for transfers between devices, layer_step(): lax.all_to_all(part_sums, 'dp', split_axis=0, concat_axis=0, tiled=True)  16.5 us
    dot_general x2, matrix products, layer_step(): jnp.dot(hidden, down_part[0], preferred_element_type=jnp.float32)  16.4 us
    all_to_all x2, starting transfers between devices, layer_step(): lax.all_to_all(outgoing, 'expert', split_axis=0, concat_axis=0, tiled=True)  12.6 us
    all_to_all x2, starting transfers between devices, layer_step(): lax.all_to_all(jnp.stack(jnp.split(lax.all_to_all(part_sums, 'dp', split_...  12 us
  transfers between devices with their start and end apart: 10, of which 6 were waited for; matrix products, arithmetic and copies ran while one was open for 21% of the time, Pallas kernels for 0%

profile of v1, /device:TPU:0, one launch (start us, length us, event | category | flops | bytes accessed | tf_op | source)
XLA Modules:
  0.0 210.7 jit_solution(16851115231067142079)
XLA Ops:
  0.0 0.8 copy.164
  0.8 209.3 %while.10 = (s32[]{:T(128)}, bf16[8,2880]{1,0:T(8,128)(2,1)S(1)}, s32[2,8,4]{1,2,0:T(4,128)}, s32[2,16]{1,0:T(2,128)}, bf16[2,1,2880]{2,0,1:T(2,128)(2,1)}, /*in...) while((s32[]{:T(128)}, bf16[8,2880]{1,0:T(8,128)(2,1)S(1)}, ...), condition=%wide.region_7.8_spmd, body=%wide.region_0.7_spmd.sunk | while | flops 1069763072 | bytes 25031192 | solution.py:100
  3.6 0.9 copy.135
  4.4 7.4 %all-to-all-start = ((bf16[16,4,2880]{2,1,0:T(4,128)(2,1)}), bf16[16,4,2880]{2,1,0:T(4,128)(2,1)S(1)}, u32[]{:S(2)}, u32[]{:S(2)}) async-start(bf16[16,4,2880]{2,1,0:T(4,128)(2,1)} %copy.135), calls=%async_computation | async-start | bytes 753664 | tf_op jit(solution)/shard_map/while/body/eval_jaxpr/all_to_all | solution.py:45
  11.8 1.2 dynamic-slice.2
  13.7 10.0 %all-to-all-done = bf16[16,4,2880]{2,1,0:T(4,128)(2,1)S(1)} async-done(((bf16[16,4,2880]{2,1,0:T(4,128)(2,1)}), bf16[16,4,2880]{2,1,0:T(4,128)(2,1)S(1)}, u32[]{:S(2)}, u32[]{:S(2)}) %all-to-all-start) | async-done | bytes 368672 | tf_op jit(solution)/shard_map/while/body/eval_jaxpr/all_to_all | solution.py:45
  23.9 11.4 %all_gather.7 = bf16[128,2880]{1,0:T(8,128)(2,1)S(1)} all-gather(bf16[64,2880]{1,0:T(8,128)(2,1)S(1)} %reshape.108), channel_id=1, replica_groups=mesh['dp'=2,'expert'=16] {'dp'}, dimensions={0}, use_global_device_ids=true | all-gather | bytes 1105920 | tf_op jit(solution)/shard_map/while/body/eval_jaxpr/all_gather | solution.py:52
  35.3 0.9 fusion.117
  36.5 4.9 %all-reduce.2 = bf16[128]{0:T(256)(128)(2,1)S(1)} all-reduce(bf16[128]{0:T(256)(128)(2,1)S(1)} %dynamic-update-slice.66), channel_id=1, replica_groups=mesh['dp'=2,'expert'=16] {'dp'}, use_global_device_ids=true, to_apply=%add | all-reduce | flops 128 | bytes 512 | tf_op jit(solution)/shard_map/while
  42.2 3.2 %all-to-all-start.3 = ((bf16[2,16,4]{1,2,0:T(4,128)(2,1)}), bf16[2,16,4]{1,2,0:T(4,128)(2,1)S(1)}, u32[]{:S(2)}, u32[]{:S(2)}) async-start(bf16[2,16,4]{1,2,0:T(4,128)(2,1)} %copy.137), calls=%async_computation.3 | async-start | bytes 4096 | tf_op jit(solution)/shard_map/while/body/eval_jaxpr/all_to_all | solution.py:82
  45.4 8.2 %fusion.100 = bf16[128,2880]{0,1:T(8,128)(2,1)S(1)} fusion(bf16[2,1,720,2880]{3,2,1,0:T(8,128)(2,1)} %get-tuple-element.130, s32[]{:T(128)} %get-tuple-element.112, bf16[128,2880]{1,0:T(8,128)(2,1)S(1)} %all_gather.7, bf16[2,1,2880,720]{2,3,1,0:T(8,128)(2,1)} %get-tuple-element.129), kind=kOutput, calls=%fused_computation.6.clone.1 | convolution fusion | flops 1062512640 | bytes 9954304 | tf_op jit(solution)/shard_map/while/body/eval_jaxpr/dot_general | solution.py:58
  54.0 1.1 reshape.109
  55.1 3.5 %all-to-all-start.1 = ((bf16[2,16,4,2880]{3,2,1,0:T(4,128)(2,1)}), bf16[2,16,4,2880]{3,2,1,0:T(4,128)(2,1)S(1)}, u32[]{:S(2)}, u32[]{:S(2)}) async-start(bf16[2,16,4,2880]{3,2,1,0:T(4,128)(2,1)} %reshape.109), calls=%async_computation.1 | async-start | bytes 1507328 | tf_op jit(solution)/shard_map/while/body/eval_jaxpr/all_to_all | solution.py:68
  59.3 8.3 %all-to-all-done.1 = bf16[2,16,4,2880]{3,2,1,0:T(4,128)(2,1)S(1)} async-done(((bf16[2,16,4,2880]{3,2,1,0:T(4,128)(2,1)}), bf16[2,16,4,2880]{3,2,1,0:T(4,128)(2,1)S(1)}, u32[]{:S(2)}, u32[]{:S(2)}) %all-to-all-start.1) | async-done | bytes 737312 | tf_op jit(solution)/shard_map/while/body/eval_jaxpr/all_to_all | solution.py:68
  67.6 3.9 %all-to-all-start.4 = ((bf16[2,16,4]{2,0,1:T(2,128)(2,1)}), bf16[2,16,4]{2,0,1:T(2,128)(2,1)S(1)}, u32[]{:S(2)}, u32[]{:S(2)}) async-start(bf16[2,16,4]{2,0,1:T(2,128)(2,1)} %copy.138), calls=%async_computation.4 | async-start | bytes 16384 | tf_op jit(solution)/shard_map/while/body/eval_jaxpr/all_to_all | solution.py:81
  81.6 6.0 %all-to-all-start.2 = ((bf16[16,2,1,4,2880]{4,3,1,2,0:T(4,128)(2,1)}), bf16[16,2,1,4,2880]{4,3,1,2,0:T(4,128)(2,1)S(1)}, u32[]{:S(2)}, u32[]{:S(2)}) async-start(bf16[16,2,1,4,2880]{4,3,1,2,0:T(4,128)(2,1)} %fusion.116), calls=%async_computation.2 | async-start | bytes 1507328 | tf_op jit(solution)/shard_map/while/body/eval_jaxpr/all_to_all | solution.py:65
  87.9 17.9 %all-to-all-done.2 = bf16[16,2,1,4,2880]{4,3,1,2,0:T(4,128)(2,1)S(1)} async-done(((bf16[16,2,1,4,2880]{4,3,1,2,0:T(4,128)(2,1)}), bf16[16,2,1,4,2880]{4,3,1,2,0:T(4,128)(2,1)S(1)}, u32[]{:S(2)}, u32[]{:S(2)}) %all-to-all-start.2) | async-done | bytes 737312 | tf_op jit(solution)/shard_map/while/body/eval_jaxpr/all_to_all | solution.py:65
  109.3 0.9 copy.135
  110.2 5.2 %all-to-all-start = ((bf16[16,4,2880]{2,1,0:T(4,128)(2,1)}), bf16[16,4,2880]{2,1,0:T(4,128)(2,1)S(1)}, u32[]{:S(2)}, u32[]{:S(2)}) async-start(bf16[16,4,2880]{2,1,0:T(4,128)(2,1)} %copy.135), calls=%async_computation | async-start | bytes 753664 | tf_op jit(solution)/shard_map/while/body/eval_jaxpr/all_to_all | solution.py:45
  115.4 1.2 dynamic-slice.2
  117.3 10.0 %all-to-all-done = bf16[16,4,2880]{2,1,0:T(4,128)(2,1)S(1)} async-done(((bf16[16,4,2880]{2,1,0:T(4,128)(2,1)}), bf16[16,4,2880]{2,1,0:T(4,128)(2,1)S(1)}, u32[]{:S(2)}, u32[]{:S(2)}) %all-to-all-start) | async-done | bytes 368672 | tf_op jit(solution)/shard_map/while/body/eval_jaxpr/all_to_all | solution.py:45
  127.4 11.4 %all_gather.7 = bf16[128,2880]{1,0:T(8,128)(2,1)S(1)} all-gather(bf16[64,2880]{1,0:T(8,128)(2,1)S(1)} %reshape.108), channel_id=1, replica_groups=mesh['dp'=2,'expert'=16] {'dp'}, dimensions={0}, use_global_device_ids=true | all-gather | bytes 1105920 | tf_op jit(solution)/shard_map/while/body/eval_jaxpr/all_gather | solution.py:52
  138.9 0.9 fusion.117
  140.0 4.9 %all-reduce.2 = bf16[128]{0:T(256)(128)(2,1)S(1)} all-reduce(bf16[128]{0:T(256)(128)(2,1)S(1)} %dynamic-update-slice.66), channel_id=1, replica_groups=mesh['dp'=2,'expert'=16] {'dp'}, use_global_device_ids=true, to_apply=%add | all-reduce | flops 128 | bytes 512 | tf_op jit(solution)/shard_map/while
  145.8 3.2 %all-to-all-start.3 = ((bf16[2,16,4]{1,2,0:T(4,128)(2,1)}), bf16[2,16,4]{1,2,0:T(4,128)(2,1)S(1)}, u32[]{:S(2)}, u32[]{:S(2)}) async-start(bf16[2,16,4]{1,2,0:T(4,128)(2,1)} %copy.137), calls=%async_computation.3 | async-start | bytes 4096 | tf_op jit(solution)/shard_map/while/body/eval_jaxpr/all_to_all | solution.py:82
  149.0 8.2 %fusion.100 = bf16[128,2880]{0,1:T(8,128)(2,1)S(1)} fusion(bf16[2,1,720,2880]{3,2,1,0:T(8,128)(2,1)} %get-tuple-element.130, s32[]{:T(128)} %get-tuple-element.112, bf16[128,2880]{1,0:T(8,128)(2,1)S(1)} %all_gather.7, bf16[2,1,2880,720]{2,3,1,0:T(8,128)(2,1)} %get-tuple-element.129), kind=kOutput, calls=%fused_computation.6.clone.1 | convolution fusion | flops 1062512640 | bytes 9954304 | tf_op jit(solution)/shard_map/while/body/eval_jaxpr/dot_general | solution.py:58
  157.6 1.1 reshape.109
  158.6 3.5 %all-to-all-start.1 = ((bf16[2,16,4,2880]{3,2,1,0:T(4,128)(2,1)}), bf16[2,16,4,2880]{3,2,1,0:T(4,128)(2,1)S(1)}, u32[]{:S(2)}, u32[]{:S(2)}) async-start(bf16[2,16,4,2880]{3,2,1,0:T(4,128)(2,1)} %reshape.109), calls=%async_computation.1 | async-start | bytes 1507328 | tf_op jit(solution)/shard_map/while/body/eval_jaxpr/all_to_all | solution.py:68
  162.9 8.3 %all-to-all-done.1 = bf16[2,16,4,2880]{3,2,1,0:T(4,128)(2,1)S(1)} async-done(((bf16[2,16,4,2880]{3,2,1,0:T(4,128)(2,1)}), bf16[2,16,4,2880]{3,2,1,0:T(4,128)(2,1)S(1)}, u32[]{:S(2)}, u32[]{:S(2)}) %all-to-all-start.1) | async-done | bytes 737312 | tf_op jit(solution)/shard_map/while/body/eval_jaxpr/all_to_all | solution.py:68
  171.1 3.9 %all-to-all-start.4 = ((bf16[2,16,4]{2,0,1:T(2,128)(2,1)}), bf16[2,16,4]{2,0,1:T(2,128)(2,1)S(1)}, u32[]{:S(2)}, u32[]{:S(2)}) async-start(bf16[2,16,4]{2,0,1:T(2,128)(2,1)} %copy.138), calls=%async_computation.4 | async-start | bytes 16384 | tf_op jit(solution)/shard_map/while/body/eval_jaxpr/all_to_all | solution.py:81
  185.2 6.0 %all-to-all-start.2 = ((bf16[16,2,1,4,2880]{4,3,1,2,0:T(4,128)(2,1)}), bf16[16,2,1,4,2880]{4,3,1,2,0:T(4,128)(2,1)S(1)}, u32[]{:S(2)}, u32[]{:S(2)}) async-start(bf16[16,2,1,4,2880]{4,3,1,2,0:T(4,128)(2,1)} %fusion.116), calls=%async_computation.2 | async-start | bytes 1507328 | tf_op jit(solution)/shard_map/while/body/eval_jaxpr/all_to_all | solution.py:65
  191.4 17.9 %all-to-all-done.2 = bf16[16,2,1,4,2880]{4,3,1,2,0:T(4,128)(2,1)S(1)} async-done(((bf16[16,2,1,4,2880]{4,3,1,2,0:T(4,128)(2,1)}), bf16[16,2,1,4,2880]{4,3,1,2,0:T(4,128)(2,1)S(1)}, u32[]{:S(2)}, u32[]{:S(2)}) %all-to-all-start.2) | async-done | bytes 737312 | tf_op jit(solution)/shard_map/while/body/eval_jaxpr/all_to_all | solution.py:65
  (92 shorter events, 32.8 us)
Async XLA Ops:
  4.4 19.3 %all-to-all-start = ((bf16[16,4,2880]{2,1,0:T(4,128)(2,1)}), bf16[16,4,2880]{2,1,0:T(4,128)(2,1)S(1)}, u32[]{:S(2)}, u32[]{:S(2)}) async-start(bf16[16,4,2880]{2,1,0:T(4,128)(2,1)} %copy.135), calls=%async_computation | async-start | bytes 753664 | tf_op jit(solution)/shard_map/while/body/eval_jaxpr/all_to_all | solution.py:45
  42.2 12.9 %all-to-all-start.3 = ((bf16[2,16,4]{1,2,0:T(4,128)(2,1)}), bf16[2,16,4]{1,2,0:T(4,128)(2,1)S(1)}, u32[]{:S(2)}, u32[]{:S(2)}) async-start(bf16[2,16,4]{1,2,0:T(4,128)(2,1)} %copy.137), calls=%async_computation.3 | async-start | bytes 4096 | tf_op jit(solution)/shard_map/while/body/eval_jaxpr/all_to_all | solution.py:82
  55.1 12.5 %all-to-all-start.1 = ((bf16[2,16,4,2880]{3,2,1,0:T(4,128)(2,1)}), bf16[2,16,4,2880]{3,2,1,0:T(4,128)(2,1)S(1)}, u32[]{:S(2)}, u32[]{:S(2)}) async-start(bf16[2,16,4,2880]{3,2,1,0:T(4,128)(2,1)} %reshape.109), calls=%async_computation.1 | async-start | bytes 1507328 | tf_op jit(solution)/shard_map/while/body/eval_jaxpr/all_to_all | solution.py:68
  67.6 14.1 %all-to-all-start.4 = ((bf16[2,16,4]{2,0,1:T(2,128)(2,1)}), bf16[2,16,4]{2,0,1:T(2,128)(2,1)S(1)}, u32[]{:S(2)}, u32[]{:S(2)}) async-start(bf16[2,16,4]{2,0,1:T(2,128)(2,1)} %copy.138), calls=%async_computation.4 | async-start | bytes 16384 | tf_op jit(solution)/shard_map/while/body/eval_jaxpr/all_to_all | solution.py:81
  81.6 24.2 %all-to-all-start.2 = ((bf16[16,2,1,4,2880]{4,3,1,2,0:T(4,128)(2,1)}), bf16[16,2,1,4,2880]{4,3,1,2,0:T(4,128)(2,1)S(1)}, u32[]{:S(2)}, u32[]{:S(2)}) async-start(bf16[16,2,1,4,2880]{4,3,1,2,0:T(4,128)(2,1)} %fusion.116), calls=%async_computation.2 | async-start | bytes 1507328 | tf_op jit(solution)/shard_map/while/body/eval_jaxpr/all_to_all | solution.py:65
  110.2 17.1 %all-to-all-start = ((bf16[16,4,2880]{2,1,0:T(4,128)(2,1)}), bf16[16,4,2880]{2,1,0:T(4,128)(2,1)S(1)}, u32[]{:S(2)}, u32[]{:S(2)}) async-start(bf16[16,4,2880]{2,1,0:T(4,128)(2,1)} %copy.135), calls=%async_computation | async-start | bytes 753664 | tf_op jit(solution)/shard_map/while/body/eval_jaxpr/all_to_all | solution.py:45
  145.8 12.9 %all-to-all-start.3 = ((bf16[2,16,4]{1,2,0:T(4,128)(2,1)}), bf16[2,16,4]{1,2,0:T(4,128)(2,1)S(1)}, u32[]{:S(2)}, u32[]{:S(2)}) async-start(bf16[2,16,4]{1,2,0:T(4,128)(2,1)} %copy.137), calls=%async_computation.3 | async-start | bytes 4096 | tf_op jit(solution)/shard_map/while/body/eval_jaxpr/all_to_all | solution.py:82
  158.6 12.5 %all-to-all-start.1 = ((bf16[2,16,4,2880]{3,2,1,0:T(4,128)(2,1)}), bf16[2,16,4,2880]{3,2,1,0:T(4,128)(2,1)S(1)}, u32[]{:S(2)}, u32[]{:S(2)}) async-start(bf16[2,16,4,2880]{3,2,1,0:T(4,128)(2,1)} %reshape.109), calls=%async_computation.1 | async-start | bytes 1507328 | tf_op jit(solution)/shard_map/while/body/eval_jaxpr/all_to_all | solution.py:68
  171.1 14.1 %all-to-all-start.4 = ((bf16[2,16,4]{2,0,1:T(2,128)(2,1)}), bf16[2,16,4]{2,0,1:T(2,128)(2,1)S(1)}, u32[]{:S(2)}, u32[]{:S(2)}) async-start(bf16[2,16,4]{2,0,1:T(2,128)(2,1)} %copy.138), calls=%async_computation.4 | async-start | bytes 16384 | tf_op jit(solution)/shard_map/while/body/eval_jaxpr/all_to_all | solution.py:81
  185.2 24.2 %all-to-all-start.2 = ((bf16[16,2,1,4,2880]{4,3,1,2,0:T(4,128)(2,1)}), bf16[16,2,1,4,2880]{4,3,1,2,0:T(4,128)(2,1)S(1)}, u32[]{:S(2)}, u32[]{:S(2)}) async-start(bf16[16,2,1,4,2880]{4,3,1,2,0:T(4,128)(2,1)} %fusion.116), calls=%async_computation.2 | async-start | bytes 1507328 | tf_op jit(solution)/shard_map/while/body/eval_jaxpr/all_to_all | solution.py:65
  210.1 0.6 copy-start
